TPU v7x, 256 devices: a whole 4x4x8 slice. The times are simulated.
256 devices in a mesh: section: 8 (over z_hi, x), dp: 32 (over z_lo, y, core).
Axes of the slice: x: 4, y: 4, z: 8 (z_hi: 2, z_lo: 4; z = z_hi * 4 + z_lo), core: 2. Of those that a mesh axis runs over, the one named last changes fastest.
Arguments:
- features: bfloat16 [1, 8, 4096, 4096], P(None, 'section', 'dp'), parts along dimension 2, may hold values from -6 to 6
- in_proj: bfloat16 [8, 4096, 512], P('section'), may hold values from -0.09375 to 0.09375
- mix_proj: bfloat16 [8, 2, 256, 256], P('section'), may hold values from -0.375 to 0.375
- out_proj: bfloat16 [8, 512, 4096], P('section'), may hold values from -0.375 to 0.375
- gate_proj: bfloat16 [8, 2, 4096], P('section'), may hold values from -0.09375 to 0.09375
- cross_bias: float32 [8, 4096], P('section'), may hold values from -3 to 3
Outputs:
- crossed: bfloat16 [1, 8, 4096, 4096], P(None, 'section', 'dp'), parts along dimension 2
There are 32 independent parts, one for each index of `dp`. A program takes and returns all parts, laid end to end along the dimension named above; an argument that names none is the same for every part. Nothing has to cross between parts.
All inputs are finite; a program needn't handle non-finite values.
Results may differ from a plain program's by a relative error of at most 0.015.
Values may be sent and summed in bfloat16 or wider, within the bound.
A program may use at most 64 MiB of HBM per device.

v0:
```python
import jax
import jax.numpy as jnp
from jax import lax
from jax.sharding import PartitionSpec as P


def from_behind(block, axis, distance):
    devices = range(lax.axis_size(axis))
    route = [(i - distance, i) for i in devices if i - distance in devices]
    return lax.ppermute(block, axis, route)


def cross_layer(current, anchor, v_mat, c_mat, u_mat, gate_mat, shift_row):
    row_count = current.shape[0]
    expert_count = c_mat.shape[0]
    rank_size = c_mat.shape[1]
    projected = jnp.dot(current, v_mat, preferred_element_type=jnp.float32)
    inner_first = (
        jnp.tanh(projected).astype(jnp.bfloat16).reshape(row_count, expert_count, rank_size)
    )
    inner_second = jnp.einsum(
        "rek,ekj->rej", inner_first, c_mat, preferred_element_type=jnp.float32
    )
    logits = lax.dot_general(
        current, gate_mat, (((1,), (1,)), ((), ())), preferred_element_type=jnp.float32
    )
    gate_values = 1.0 / jnp.sum(jnp.exp(logits[:, None, :] - logits[:, :, None]), axis=2)
    blended = (gate_values[:, :, None] * jnp.tanh(inner_second)).astype(jnp.bfloat16)
    blended = blended.reshape(row_count, expert_count * rank_size)
    crossed = jnp.dot(blended, u_mat, preferred_element_type=jnp.float32)
    updated = current.astype(jnp.float32) + anchor.astype(jnp.float32) * (crossed + shift_row)
    return updated.astype(jnp.bfloat16)


def per_device(features, in_proj, mix_proj, out_proj, gate_proj, cross_bias):
    section_count = lax.axis_size("section")
    position = lax.axis_index("section")
    pieces = 2
    local_micro = features.shape[0]
    row_count = features.shape[2]
    feature_count = features.shape[3]
    piece_rows = row_count // pieces
    everyone = lax.all_gather(features, "section", axis=1, tiled=True)
    all_units = everyone.reshape(local_micro * section_count * pieces, piece_rows, feature_count)
    unit_count = all_units.shape[0]
    step_count = unit_count + section_count - 1
    v_mat = in_proj[0]
    c_mat = mix_proj[0]
    u_mat = out_proj[0]
    gate_mat = gate_proj[0]
    shift_row = cross_bias[0]

    def apply_layer(current, anchor):
        return cross_layer(current, anchor, v_mat, c_mat, u_mat, gate_mat, shift_row)

    def keep_input(current, anchor):
        return current

    def advance(carried, moment):
        incoming, outgoing, collected = carried
        unit_here = moment - position
        active = (unit_here >= 0) & (unit_here < unit_count)
        anchor = lax.dynamic_index_in_dim(
            all_units, jnp.clip(unit_here, 0, unit_count - 1), 0, keepdims=False
        )
        current = jnp.where(position == 0, anchor, incoming)
        result = lax.cond(active, apply_layer, keep_input, current, anchor)
        outgoing = jnp.where(position == section_count - 1, result, outgoing)
        held_unit = moment + position - 2 * section_count + 2
        arrived = (
            (held_unit >= 0)
            & (held_unit < unit_count)
            & (held_unit // pieces % section_count == position)
        )
        held_safe = jnp.clip(held_unit, 0, unit_count - 1)
        slot_index = held_safe // pieces // section_count * pieces + held_safe % pieces
        previous = lax.dynamic_index_in_dim(collected, slot_index, 0, keepdims=False)
        collected = lax.dynamic_update_index_in_dim(
            collected, jnp.where(arrived, outgoing, previous), slot_index, 0
        )
        return (result, outgoing, collected)

    def forward_step(carried, moment):
        result, outgoing, collected = advance(carried, moment)
        incoming = from_behind(result, "section", 1)
        return ((incoming, outgoing, collected), None)

    def cycle_step(carried, moment):
        moved, _ = forward_step(carried, moment)
        incoming, outgoing, collected = moved
        outgoing = from_behind(outgoing, "section", -1)
        return ((incoming, outgoing, collected), None)

    blank = jnp.zeros((piece_rows, feature_count), jnp.bfloat16)
    holding = jnp.zeros((local_micro * pieces, piece_rows, feature_count), jnp.bfloat16)
    carried, _ = lax.scan(
        forward_step, (blank, blank, holding), jnp.arange(0, section_count - 1, dtype=jnp.int32)
    )
    carried, _ = lax.scan(
        cycle_step, carried, jnp.arange(section_count - 1, step_count - 1, dtype=jnp.int32)
    )
    _, _, collected = advance(carried, jnp.int32(step_count - 1))
    return collected.reshape(local_micro, 1, row_count, feature_count)


def solution(mesh):
    placed = (
        P(None, "section", "dp", None),
        P("section", None, None),
        P("section", None, None, None),
        P("section", None, None),
        P("section", None, None),
        P("section", None),
    )
    return jax.shard_map(
        per_device,
        mesh=mesh,
        in_specs=placed,
        out_specs=P(None, "section", "dp", None),
        check_vma=False,
    )
```

profile of v0, /device:TPU:160, one launch (start us, length us, event | category | flops | bytes accessed | tf_op | source)
XLA Modules:
  0.0 966.1 jit_solution(16218471225976274042)
XLA Ops:
  7.3 171.0 %all-gather.2.cloned.1.call-done = bf16[1,8,128,4096]{3,2,0,1:T(8,128)(2,1)} async-done(((bf16[1,1,128,4096]{3,2,0,1:T(8,128)(2,1)}), bf16[1,8,128,4096]{3,2,0,1:T(8,128)(2,1)}) %all-gather.2.cloned.1.call-update) | async-done | bytes 8388624 | tf_op jit(solution)/shard_map/all_gather | solution.py:43
  179.5 250.9 %while.40 = (s32[]{:T(128)}, bf16[64,4096]{1,0:T(8,128)(2,1)S(1)}, bf16[64,4096]{1,0:T(8,128)(2,1)S(1)}, bf16[2,64,4096]{2,1,0:T(8,128)(2,1)}, s32[7]{0:T(128)S(...) while((s32[]{:T(128)}, bf16[64,4096]{1,0:T(8,128)(2,1)S(1)}, ...), condition=%wide.region_4.5_spmd.clone, body=%wide.region_0.4_spmd.clone.sunk | while | flops 557416960 | bytes 37524112 | solution.py:96
  187.0 31.3 %collective-permute-done.2 = bf16[64,4096]{1,0:T(8,128)(2,1)S(1)} collective-permute-done((bf16[64,4096]{1,0:T(8,128)(2,1)S(1)}, bf16[64,4096]{1,0:T(8,128)(2,1)S(1)}, u32[]{:S(2)}, u32[]{:S(2)}) %collective-permute-start.2) | collective-permute-done | bytes 524320 | tf_op jit(solution)/shard_map/while/body/eval_jaxpr/ppermute | solution.py:10
  225.5 36.1 %collective-permute-done.2 = bf16[64,4096]{1,0:T(8,128)(2,1)S(1)} collective-permute-done((bf16[64,4096]{1,0:T(8,128)(2,1)S(1)}, bf16[64,4096]{1,0:T(8,128)(2,1)S(1)}, u32[]{:S(2)}, u32[]{:S(2)}) %collective-permute-start.2) | collective-permute-done | bytes 524320 | tf_op jit(solution)/shard_map/while/body/eval_jaxpr/ppermute | solution.py:10
  268.8 25.8 %collective-permute-done.2 = bf16[64,4096]{1,0:T(8,128)(2,1)S(1)} collective-permute-done((bf16[64,4096]{1,0:T(8,128)(2,1)S(1)}, bf16[64,4096]{1,0:T(8,128)(2,1)S(1)}, u32[]{:S(2)}, u32[]{:S(2)}) %collective-permute-start.2) | collective-permute-done | bytes 524320 | tf_op jit(solution)/shard_map/while/body/eval_jaxpr/ppermute | solution.py:10
  301.8 23.0 %collective-permute-done.2 = bf16[64,4096]{1,0:T(8,128)(2,1)S(1)} collective-permute-done((bf16[64,4096]{1,0:T(8,128)(2,1)S(1)}, bf16[64,4096]{1,0:T(8,128)(2,1)S(1)}, u32[]{:S(2)}, u32[]{:S(2)}) %collective-permute-start.2) | collective-permute-done | bytes 524320 | tf_op jit(solution)/shard_map/while/body/eval_jaxpr/ppermute | solution.py:10
  336.9 27.7 %collective-permute-done.2 = bf16[64,4096]{1,0:T(8,128)(2,1)S(1)} collective-permute-done((bf16[64,4096]{1,0:T(8,128)(2,1)S(1)}, bf16[64,4096]{1,0:T(8,128)(2,1)S(1)}, u32[]{:S(2)}, u32[]{:S(2)}) %collective-permute-start.2) | collective-permute-done | bytes 524320 | tf_op jit(solution)/shard_map/while/body/eval_jaxpr/ppermute | solution.py:10
  376.6 21.3 %collective-permute-done.2 = bf16[64,4096]{1,0:T(8,128)(2,1)S(1)} collective-permute-done((bf16[64,4096]{1,0:T(8,128)(2,1)S(1)}, bf16[64,4096]{1,0:T(8,128)(2,1)S(1)}, u32[]{:S(2)}, u32[]{:S(2)}) %collective-permute-start.2) | collective-permute-done | bytes 524320 | tf_op jit(solution)/shard_map/while/body/eval_jaxpr/ppermute | solution.py:10
  409.9 20.4 %collective-permute-done.2 = bf16[64,4096]{1,0:T(8,128)(2,1)S(1)} collective-permute-done((bf16[64,4096]{1,0:T(8,128)(2,1)S(1)}, bf16[64,4096]{1,0:T(8,128)(2,1)S(1)}, u32[]{:S(2)}, u32[]{:S(2)}) %collective-permute-start.2) | collective-permute-done | bytes 524320 | tf_op jit(solution)/shard_map/while/body/eval_jaxpr/ppermute | solution.py:10
  430.3 525.7 %while.39 = (s32[]{:T(128)}, bf16[64,4096]{1,0:T(8,128)(2,1)S(1)}, bf16[64,4096]{1,0:T(8,128)(2,1)S(1)}, bf16[2,64,4096]{2,1,0:T(8,128)(2,1)}, s32[15]{0:T(128)S...) while((s32[]{:T(128)}, bf16[64,4096]{1,0:T(8,128)(2,1)S(1)}, ...), condition=%wide.region_9.10_spmd, body=%wide.region_5.9_spmd.sunk | while | flops 557154816 | bytes 39621292 | solution.py:99
  446.2 12.7 %collective-permute-done.1 = bf16[64,4096]{1,0:T(8,128)(2,1)S(1)} collective-permute-done((bf16[64,4096]{1,0:T(8,128)(2,1)S(1)}, bf16[64,4096]{1,0:T(8,128)(2,1)S(1)}, u32[]{:S(2)}, u32[]{:S(2)}) %collective-permute-start.1) | collective-permute-done | bytes 524320 | tf_op jit(solution)/shard_map/while/body/eval_jaxpr/ppermute | solution.py:10
  459.0 10.1 %collective-permute-done = bf16[64,4096]{1,0:T(8,128)(2,1)S(1)} collective-permute-done((bf16[64,4096]{1,0:T(8,128)(2,1)S(1)}, bf16[64,4096]{1,0:T(8,128)(2,1)S(1)}, u32[]{:S(2)}, u32[]{:S(2)}) %collective-permute-start) | collective-permute-done | bytes 524320 | tf_op jit(solution)/shard_map/while/body/eval_jaxpr/ppermute | solution.py:10
  485.0 13.6 %collective-permute-done.1 = bf16[64,4096]{1,0:T(8,128)(2,1)S(1)} collective-permute-done((bf16[64,4096]{1,0:T(8,128)(2,1)S(1)}, bf16[64,4096]{1,0:T(8,128)(2,1)S(1)}, u32[]{:S(2)}, u32[]{:S(2)}) %collective-permute-start.1) | collective-permute-done | bytes 524320 | tf_op jit(solution)/shard_map/while/body/eval_jaxpr/ppermute | solution.py:10
  498.6 10.1 %collective-permute-done = bf16[64,4096]{1,0:T(8,128)(2,1)S(1)} collective-permute-done((bf16[64,4096]{1,0:T(8,128)(2,1)S(1)}, bf16[64,4096]{1,0:T(8,128)(2,1)S(1)}, u32[]{:S(2)}, u32[]{:S(2)}) %collective-permute-start) | collective-permute-done | bytes 524320 | tf_op jit(solution)/shard_map/while/body/eval_jaxpr/ppermute | solution.py:10
  524.6 17.9 %collective-permute-done.1 = bf16[64,4096]{1,0:T(8,128)(2,1)S(1)} collective-permute-done((bf16[64,4096]{1,0:T(8,128)(2,1)S(1)}, bf16[64,4096]{1,0:T(8,128)(2,1)S(1)}, u32[]{:S(2)}, u32[]{:S(2)}) %collective-permute-start.1) | collective-permute-done | bytes 524320 | tf_op jit(solution)/shard_map/while/body/eval_jaxpr/ppermute | solution.py:10
  542.5 10.4 %collective-permute-done = bf16[64,4096]{1,0:T(8,128)(2,1)S(1)} collective-permute-done((bf16[64,4096]{1,0:T(8,128)(2,1)S(1)}, bf16[64,4096]{1,0:T(8,128)(2,1)S(1)}, u32[]{:S(2)}, u32[]{:S(2)}) %collective-permute-start) | collective-permute-done | bytes 524320 | tf_op jit(solution)/shard_map/while/body/eval_jaxpr/ppermute | solution.py:10
  602.9 12.8 %collective-permute-done.1 = bf16[64,4096]{1,0:T(8,128)(2,1)S(1)} collective-permute-done((bf16[64,4096]{1,0:T(8,128)(2,1)S(1)}, bf16[64,4096]{1,0:T(8,128)(2,1)S(1)}, u32[]{:S(2)}, u32[]{:S(2)}) %collective-permute-start.1) | collective-permute-done | bytes 524320 | tf_op jit(solution)/shard_map/while/body/eval_jaxpr/ppermute | solution.py:10
  615.7 10.1 %collective-permute-done = bf16[64,4096]{1,0:T(8,128)(2,1)S(1)} collective-permute-done((bf16[64,4096]{1,0:T(8,128)(2,1)S(1)}, bf16[64,4096]{1,0:T(8,128)(2,1)S(1)}, u32[]{:S(2)}, u32[]{:S(2)}) %collective-permute-start) | collective-permute-done | bytes 524320 | tf_op jit(solution)/shard_map/while/body/eval_jaxpr/ppermute | solution.py:10
  641.8 17.2 %collective-permute-done.1 = bf16[64,4096]{1,0:T(8,128)(2,1)S(1)} collective-permute-done((bf16[64,4096]{1,0:T(8,128)(2,1)S(1)}, bf16[64,4096]{1,0:T(8,128)(2,1)S(1)}, u32[]{:S(2)}, u32[]{:S(2)}) %collective-permute-start.1) | collective-permute-done | bytes 524320 | tf_op jit(solution)/shard_map/while/body/eval_jaxpr/ppermute | solution.py:10
  658.9 10.4 %collective-permute-done = bf16[64,4096]{1,0:T(8,128)(2,1)S(1)} collective-permute-done((bf16[64,4096]{1,0:T(8,128)(2,1)S(1)}, bf16[64,4096]{1,0:T(8,128)(2,1)S(1)}, u32[]{:S(2)}, u32[]{:S(2)}) %collective-permute-start) | collective-permute-done | bytes 524320 | tf_op jit(solution)/shard_map/while/body/eval_jaxpr/ppermute | solution.py:10
  685.2 9.9 %collective-permute-done.1 = bf16[64,4096]{1,0:T(8,128)(2,1)S(1)} collective-permute-done((bf16[64,4096]{1,0:T(8,128)(2,1)S(1)}, bf16[64,4096]{1,0:T(8,128)(2,1)S(1)}, u32[]{:S(2)}, u32[]{:S(2)}) %collective-permute-start.1) | collective-permute-done | bytes 524320 | tf_op jit(solution)/shard_map/while/body/eval_jaxpr/ppermute | solution.py:10
  719.0 18.1 %collective-permute-done.1 = bf16[64,4096]{1,0:T(8,128)(2,1)S(1)} collective-permute-done((bf16[64,4096]{1,0:T(8,128)(2,1)S(1)}, bf16[64,4096]{1,0:T(8,128)(2,1)S(1)}, u32[]{:S(2)}, u32[]{:S(2)}) %collective-permute-start.1) | collective-permute-done | bytes 524320 | tf_op jit(solution)/shard_map/while/body/eval_jaxpr/ppermute | solution.py:10
  737.0 10.1 %collective-permute-done = bf16[64,4096]{1,0:T(8,128)(2,1)S(1)} collective-permute-done((bf16[64,4096]{1,0:T(8,128)(2,1)S(1)}, bf16[64,4096]{1,0:T(8,128)(2,1)S(1)}, u32[]{:S(2)}, u32[]{:S(2)}) %collective-permute-start) | collective-permute-done | bytes 524320 | tf_op jit(solution)/shard_map/while/body/eval_jaxpr/ppermute | solution.py:10
  770.5 10.4 %collective-permute-done = bf16[64,4096]{1,0:T(8,128)(2,1)S(1)} collective-permute-done((bf16[64,4096]{1,0:T(8,128)(2,1)S(1)}, bf16[64,4096]{1,0:T(8,128)(2,1)S(1)}, u32[]{:S(2)}, u32[]{:S(2)}) %collective-permute-start) | collective-permute-done | bytes 524320 | tf_op jit(solution)/shard_map/while/body/eval_jaxpr/ppermute | solution.py:10
  (414 shorter events, 466.2 us)
Async XLA Ops:
  6.5 171.8 %all-gather.2.cloned.1.call-start = ((), (), s32[]{:S(2)}) async-start(), calls=%async_computation | async-start | bytes 9437184 | tf_op jit(solution)/shard_map/all_gather | solution.py:43
  181.9 36.4 %collective-permute-start.2 = (bf16[64,4096]{1,0:T(8,128)(2,1)S(1)}, bf16[64,4096]{1,0:T(8,128)(2,1)S(1)}, u32[]{:S(2)}, u32[]{:S(2)}) collective-permute-start(bf16[64,4096]{1,0:T(8,128)(2,1)S(1)} %get-tuple-element.1181), channel_id=1, source_target_pairs={{0,32},{32,64},{64,96},{96,128},{128,160},{160,192},{192,224},{1,3... | collective-permute-start | bytes 1572872 | tf_op jit(solution)/shard_map/while/body/eval_jaxpr/ppermute | solution.py:10
  220.7 40.9 %collective-permute-start.2 = (bf16[64,4096]{1,0:T(8,128)(2,1)S(1)}, bf16[64,4096]{1,0:T(8,128)(2,1)S(1)}, u32[]{:S(2)}, u32[]{:S(2)}) collective-permute-start(bf16[64,4096]{1,0:T(8,128)(2,1)S(1)} %get-tuple-element.1181), channel_id=1, source_target_pairs={{0,32},{32,64},{64,96},{96,128},{128,160},{160,192},{192,224},{1,3... | collective-permute-start | bytes 1572872 | tf_op jit(solution)/shard_map/while/body/eval_jaxpr/ppermute | solution.py:10
  264.0 30.6 %collective-permute-start.2 = (bf16[64,4096]{1,0:T(8,128)(2,1)S(1)}, bf16[64,4096]{1,0:T(8,128)(2,1)S(1)}, u32[]{:S(2)}, u32[]{:S(2)}) collective-permute-start(bf16[64,4096]{1,0:T(8,128)(2,1)S(1)} %get-tuple-element.1181), channel_id=1, source_target_pairs={{0,32},{32,64},{64,96},{96,128},{128,160},{160,192},{192,224},{1,3... | collective-permute-start | bytes 1572872 | tf_op jit(solution)/shard_map/while/body/eval_jaxpr/ppermute | solution.py:10
  297.0 27.8 %collective-permute-start.2 = (bf16[64,4096]{1,0:T(8,128)(2,1)S(1)}, bf16[64,4096]{1,0:T(8,128)(2,1)S(1)}, u32[]{:S(2)}, u32[]{:S(2)}) collective-permute-start(bf16[64,4096]{1,0:T(8,128)(2,1)S(1)} %get-tuple-element.1181), channel_id=1, source_target_pairs={{0,32},{32,64},{64,96},{96,128},{128,160},{160,192},{192,224},{1,3... | collective-permute-start | bytes 1572872 | tf_op jit(solution)/shard_map/while/body/eval_jaxpr/ppermute | solution.py:10
  332.0 32.6 %collective-permute-start.2 = (bf16[64,4096]{1,0:T(8,128)(2,1)S(1)}, bf16[64,4096]{1,0:T(8,128)(2,1)S(1)}, u32[]{:S(2)}, u32[]{:S(2)}) collective-permute-start(bf16[64,4096]{1,0:T(8,128)(2,1)S(1)} %get-tuple-element.1181), channel_id=1, source_target_pairs={{0,32},{32,64},{64,96},{96,128},{128,160},{160,192},{192,224},{1,3... | collective-permute-start | bytes 1572872 | tf_op jit(solution)/shard_map/while/body/eval_jaxpr/ppermute | solution.py:10
  371.8 26.1 %collective-permute-start.2 = (bf16[64,4096]{1,0:T(8,128)(2,1)S(1)}, bf16[64,4096]{1,0:T(8,128)(2,1)S(1)}, u32[]{:S(2)}, u32[]{:S(2)}) collective-permute-start(bf16[64,4096]{1,0:T(8,128)(2,1)S(1)} %get-tuple-element.1181), channel_id=1, source_target_pairs={{0,32},{32,64},{64,96},{96,128},{128,160},{160,192},{192,224},{1,3... | collective-permute-start | bytes 1572872 | tf_op jit(solution)/shard_map/while/body/eval_jaxpr/ppermute | solution.py:10
  405.1 25.3 %collective-permute-start.2 = (bf16[64,4096]{1,0:T(8,128)(2,1)S(1)}, bf16[64,4096]{1,0:T(8,128)(2,1)S(1)}, u32[]{:S(2)}, u32[]{:S(2)}) collective-permute-start(bf16[64,4096]{1,0:T(8,128)(2,1)S(1)} %get-tuple-element.1181), channel_id=1, source_target_pairs={{0,32},{32,64},{64,96},{96,128},{128,160},{160,192},{192,224},{1,3... | collective-permute-start | bytes 1572872 | tf_op jit(solution)/shard_map/while/body/eval_jaxpr/ppermute | solution.py:10
  442.3 26.8 %collective-permute-start = (bf16[64,4096]{1,0:T(8,128)(2,1)S(1)}, bf16[64,4096]{1,0:T(8,128)(2,1)S(1)}, u32[]{:S(2)}, u32[]{:S(2)}) collective-permute-start(bf16[64,4096]{1,0:T(8,128)(2,1)S(1)} %get-tuple-element.1180), channel_id=1, source_target_pairs={{0,32},{32,64},{64,96},{96,128},{128,160},{160,192},{192,224},{1,3... | collective-permute-start | bytes 1572872 | tf_op jit(solution)/shard_map/while/body/eval_jaxpr/ppermute | solution.py:10
  479.2 19.4 %collective-permute-start.1 = (bf16[64,4096]{1,0:T(8,128)(2,1)S(1)}, bf16[64,4096]{1,0:T(8,128)(2,1)S(1)}, u32[]{:S(2)}, u32[]{:S(2)}) collective-permute-start(bf16[64,4096]{1,0:T(8,128)(2,1)S(1)} %get-tuple-element.1015), channel_id=1, source_target_pairs={{32,0},{64,32},{96,64},{128,96},{160,128},{192,160},{224,192},{33,... | collective-permute-start | bytes 1572872 | tf_op jit(solution)/shard_map/while/body/eval_jaxpr/ppermute | solution.py:10
  481.1 27.6 %collective-permute-start = (bf16[64,4096]{1,0:T(8,128)(2,1)S(1)}, bf16[64,4096]{1,0:T(8,128)(2,1)S(1)}, u32[]{:S(2)}, u32[]{:S(2)}) collective-permute-start(bf16[64,4096]{1,0:T(8,128)(2,1)S(1)} %get-tuple-element.1180), channel_id=1, source_target_pairs={{0,32},{32,64},{64,96},{96,128},{128,160},{160,192},{192,224},{1,3... | collective-permute-start | bytes 1572872 | tf_op jit(solution)/shard_map/while/body/eval_jaxpr/ppermute | solution.py:10
  518.8 23.8 %collective-permute-start.1 = (bf16[64,4096]{1,0:T(8,128)(2,1)S(1)}, bf16[64,4096]{1,0:T(8,128)(2,1)S(1)}, u32[]{:S(2)}, u32[]{:S(2)}) collective-permute-start(bf16[64,4096]{1,0:T(8,128)(2,1)S(1)} %get-tuple-element.1015), channel_id=1, source_target_pairs={{32,0},{64,32},{96,64},{128,96},{160,128},{192,160},{224,192},{33,... | collective-permute-start | bytes 1572872 | tf_op jit(solution)/shard_map/while/body/eval_jaxpr/ppermute | solution.py:10
  520.7 32.2 %collective-permute-start = (bf16[64,4096]{1,0:T(8,128)(2,1)S(1)}, bf16[64,4096]{1,0:T(8,128)(2,1)S(1)}, u32[]{:S(2)}, u32[]{:S(2)}) collective-permute-start(bf16[64,4096]{1,0:T(8,128)(2,1)S(1)} %get-tuple-element.1180), channel_id=1, source_target_pairs={{0,32},{32,64},{64,96},{96,128},{128,160},{160,192},{192,224},{1,3... | collective-permute-start | bytes 1572872 | tf_op jit(solution)/shard_map/while/body/eval_jaxpr/ppermute | solution.py:10
  564.9 22.1 %collective-permute-start = (bf16[64,4096]{1,0:T(8,128)(2,1)S(1)}, bf16[64,4096]{1,0:T(8,128)(2,1)S(1)}, u32[]{:S(2)}, u32[]{:S(2)}) collective-permute-start(bf16[64,4096]{1,0:T(8,128)(2,1)S(1)} %get-tuple-element.1180), channel_id=1, source_target_pairs={{0,32},{32,64},{64,96},{96,128},{128,160},{160,192},{192,224},{1,3... | collective-permute-start | bytes 1572872 | tf_op jit(solution)/shard_map/while/body/eval_jaxpr/ppermute | solution.py:10
  599.0 26.9 %collective-permute-start = (bf16[64,4096]{1,0:T(8,128)(2,1)S(1)}, bf16[64,4096]{1,0:T(8,128)(2,1)S(1)}, u32[]{:S(2)}, u32[]{:S(2)}) collective-permute-start(bf16[64,4096]{1,0:T(8,128)(2,1)S(1)} %get-tuple-element.1180), channel_id=1, source_target_pairs={{0,32},{32,64},{64,96},{96,128},{128,160},{160,192},{192,224},{1,3... | collective-permute-start | bytes 1572872 | tf_op jit(solution)/shard_map/while/body/eval_jaxpr/ppermute | solution.py:10
  635.9 23.0 %collective-permute-start.1 = (bf16[64,4096]{1,0:T(8,128)(2,1)S(1)}, bf16[64,4096]{1,0:T(8,128)(2,1)S(1)}, u32[]{:S(2)}, u32[]{:S(2)}) collective-permute-start(bf16[64,4096]{1,0:T(8,128)(2,1)S(1)} %get-tuple-element.1015), channel_id=1, source_target_pairs={{32,0},{64,32},{96,64},{128,96},{160,128},{192,160},{224,192},{33,... | collective-permute-start | bytes 1572872 | tf_op jit(solution)/shard_map/while/body/eval_jaxpr/ppermute | solution.py:10
  637.8 31.5 %collective-permute-start = (bf16[64,4096]{1,0:T(8,128)(2,1)S(1)}, bf16[64,4096]{1,0:T(8,128)(2,1)S(1)}, u32[]{:S(2)}, u32[]{:S(2)}) collective-permute-start(bf16[64,4096]{1,0:T(8,128)(2,1)S(1)} %get-tuple-element.1180), channel_id=1, source_target_pairs={{0,32},{32,64},{64,96},{96,128},{128,160},{160,192},{192,224},{1,3... | collective-permute-start | bytes 1572872 | tf_op jit(solution)/shard_map/while/body/eval_jaxpr/ppermute | solution.py:10
  681.3 21.8 %collective-permute-start = (bf16[64,4096]{1,0:T(8,128)(2,1)S(1)}, bf16[64,4096]{1,0:T(8,128)(2,1)S(1)}, u32[]{:S(2)}, u32[]{:S(2)}) collective-permute-start(bf16[64,4096]{1,0:T(8,128)(2,1)S(1)} %get-tuple-element.1180), channel_id=1, source_target_pairs={{0,32},{32,64},{64,96},{96,128},{128,160},{160,192},{192,224},{1,3... | collective-permute-start | bytes 1572872 | tf_op jit(solution)/shard_map/while/body/eval_jaxpr/ppermute | solution.py:10
  713.1 23.9 %collective-permute-start.1 = (bf16[64,4096]{1,0:T(8,128)(2,1)S(1)}, bf16[64,4096]{1,0:T(8,128)(2,1)S(1)}, u32[]{:S(2)}, u32[]{:S(2)}) collective-permute-start(bf16[64,4096]{1,0:T(8,128)(2,1)S(1)} %get-tuple-element.1015), channel_id=1, source_target_pairs={{32,0},{64,32},{96,64},{128,96},{160,128},{192,160},{224,192},{33,... | collective-permute-start | bytes 1572872 | tf_op jit(solution)/shard_map/while/body/eval_jaxpr/ppermute | solution.py:10
  715.0 32.1 %collective-permute-start = (bf16[64,4096]{1,0:T(8,128)(2,1)S(1)}, bf16[64,4096]{1,0:T(8,128)(2,1)S(1)}, u32[]{:S(2)}, u32[]{:S(2)}) collective-permute-start(bf16[64,4096]{1,0:T(8,128)(2,1)S(1)} %get-tuple-element.1180), channel_id=1, source_target_pairs={{0,32},{32,64},{64,96},{96,128},{128,160},{160,192},{192,224},{1,3... | collective-permute-start | bytes 1572872 | tf_op jit(solution)/shard_map/while/body/eval_jaxpr/ppermute | solution.py:10
  759.1 21.8 %collective-permute-start = (bf16[64,4096]{1,0:T(8,128)(2,1)S(1)}, bf16[64,4096]{1,0:T(8,128)(2,1)S(1)}, u32[]{:S(2)}, u32[]{:S(2)}) collective-permute-start(bf16[64,4096]{1,0:T(8,128)(2,1)S(1)} %get-tuple-element.1180), channel_id=1, source_target_pairs={{0,32},{32,64},{64,96},{96,128},{128,160},{160,192},{192,224},{1,3... | collective-permute-start | bytes 1572872 | tf_op jit(solution)/shard_map/while/body/eval_jaxpr/ppermute | solution.py:10
  792.8 20.9 %collective-permute-start = (bf16[64,4096]{1,0:T(8,128)(2,1)S(1)}, bf16[64,4096]{1,0:T(8,128)(2,1)S(1)}, u32[]{:S(2)}, u32[]{:S(2)}) collective-permute-start(bf16[64,4096]{1,0:T(8,128)(2,1)S(1)} %get-tuple-element.1180), channel_id=1, source_target_pairs={{0,32},{32,64},{64,96},{96,128},{128,160},{160,192},{192,224},{1,3... | collective-permute-start | bytes 1572872 | tf_op jit(solution)/shard_map/while/body/eval_jaxpr/ppermute | solution.py:10
  825.7 20.0 %collective-permute-start = (bf16[64,4096]{1,0:T(8,128)(2,1)S(1)}, bf16[64,4096]{1,0:T(8,128)(2,1)S(1)}, u32[]{:S(2)}, u32[]{:S(2)}) collective-permute-start(bf16[64,4096]{1,0:T(8,128)(2,1)S(1)} %get-tuple-element.1180), channel_id=1, source_target_pairs={{0,32},{32,64},{64,96},{96,128},{128,160},{160,192},{192,224},{1,3... | collective-permute-start | bytes 1572872 | tf_op jit(solution)/shard_map/while/body/eval_jaxpr/ppermute | solution.py:10
  857.7 19.2 %collective-permute-start = (bf16[64,4096]{1,0:T(8,128)(2,1)S(1)}, bf16[64,4096]{1,0:T(8,128)(2,1)S(1)}, u32[]{:S(2)}, u32[]{:S(2)}) collective-permute-start(bf16[64,4096]{1,0:T(8,128)(2,1)S(1)} %get-tuple-element.1180), channel_id=1, source_target_pairs={{0,32},{32,64},{64,96},{96,128},{128,160},{160,192},{192,224},{1,3... | collective-permute-start | bytes 1572872 | tf_op jit(solution)/shard_map/while/body/eval_jaxpr/ppermute | solution.py:10
  (78 other events, 439.7 us)
Sparse Core Ops, SparseCore 0:
  10.0 168.3 all-gather.1
where the time goes:
time: 970 us; the launch traced here: 966 us
  waiting for transfers between devices  654 us (67%)
  starting transfers between devices  101 us (10%)
  matrix products  73.6 us (8%)
  other arithmetic  50.4 us (5%)
  local copies, waits for them, and re-layouts  40.5 us (4%)
  loops' own time  32.8 us (3%)
  between operations  13.5 us (1%)
    ppermute x37, waiting for transfers between devices, from_behind(): return lax.ppermute(block, axis, route)  482 us
    all_gather x1, waiting for transfers between devices, per_device(): everyone = lax.all_gather(features, 'section', axis=1, tiled=True)  171 us
    ppermute x37, starting transfers between devices, from_behind(): return lax.ppermute(block, axis, route)  101 us
    dot_general x16, matrix products, cross_layer(): projected = jnp.dot(current, v_mat, preferred_element_type=jnp.float32)  51 us
    select_n x23, other arithmetic, advance(): current = jnp.where(position == 0, anchor, incoming)  25.7 us
    dynamic_slice x23, local copies, waits for them, and re-layouts, advance(): lax.dynamic_index_in_dim(collected, slot_index, 0, keepdims=False)  24.9 us
    dynamic_update_slice x23, other arithmetic, advance(): lax.dynamic_update_index_in_dim(collected, jnp.where(arrived, outgoing, p...  24 us
    another operation x1, loops' own time, per_device(): lax.scan(cycle_step, carried, jnp.arange(section_count - 1, step_count -...  21 us
  transfers between devices with their start and end apart: 38, of which 38 were waited for; matrix products, arithmetic and copies ran while one was open for 2% of the time, Pallas kernels for 0%

commit v1 on v0

--- a/solution.py
+++ b/solution.py
@@ -1,7 +1,18 @@
+import functools
 import jax
 import jax.numpy as jnp
 from jax import lax
 from jax.sharding import PartitionSpec as P
+
+
+def sums_all_number(local_values, device_axis):
+    tall = jnp.stack([local_values for _ in range(lax.axis_size(device_axis))])
+    t_next = lax.all_to_all(tall, device_axis, split_axis=0, concat_axis=0)
+    response = jnp.concatenate(t_next, axis=1)
+    return response
+
+
+remake_the_shelves = functools.partial(sums_all_number, device_axis="section")
 
 
 def from_behind(block, axis, distance):
@@ -40,7 +51,7 @@
     row_count = features.shape[2]
     feature_count = features.shape[3]
     piece_rows = row_count // pieces
-    everyone = lax.all_gather(features, "section", axis=1, tiled=True)
+    everyone = remake_the_shelves(features)
     all_units = everyone.reshape(local_micro * section_count * pieces, piece_rows, feature_count)
     unit_count = all_units.shape[0]
     step_count = unit_count + section_count - 1

time: 970 us -> 932 us (0.961)
  waiting for transfers between devices: 654 us -> 592 us
  starting transfers between devices: 101 us -> 131 us
  between operations: 13.5 us -> 0.05 us
    all_gather x1 -> x0, waiting for transfers between devices: 171 us -> none  [per_device(): everyone = lax.all_gather(features, 'section', axis=1, tiled=True)]
    all_to_all x0 -> x1, waiting for transfers between devices: none -> 164 us  [sums_all_number(): t_next = lax.all_to_all(tall, device_axis, split_axis=0, concat_axis=0)]
    ppermute x37, waiting for transfers between devices: 482 us -> 428 us  [from_behind(): return lax.ppermute(block, axis, route)]
    ppermute x37, starting transfers between devices: 101 us -> 121 us  [from_behind(): return lax.ppermute(block, axis, route)]
    all_to_all x0 -> x1, starting transfers between devices: none -> 9.8 us  [sums_all_number(): t_next = lax.all_to_all(tall, device_axis, split_axis=0, concat_axis=0)]
where the time goes in v1:
time: 932 us; the launch traced here: 923 us
  waiting for transfers between devices  592 us (64%)
  starting transfers between devices  131 us (14%)
  matrix products  73.6 us (8%)
  other arithmetic  50.4 us (5%)
  local copies, waits for them, and re-layouts  44.9 us (5%)
  loops' own time  31.4 us (3%)
    ppermute x37, waiting for transfers between devices, from_behind(): return lax.ppermute(block, axis, route)  428 us
    all_to_all x1, waiting for transfers between devices, sums_all_number(): t_next = lax.all_to_all(tall, device_axis, split_axis=0, concat_axis=0)  164 us
    ppermute x37, starting transfers between devices, from_behind(): return lax.ppermute(block, axis, route)  121 us
    dot_general x16, matrix products, cross_layer(): projected = jnp.dot(current, v_mat, preferred_element_type=jnp.float32)  51 us
    select_n x23, other arithmetic, advance(): current = jnp.where(position == 0, anchor, incoming)  25.7 us
    dynamic_slice x23, local copies, waits for them, and re-layouts, advance(): lax.dynamic_index_in_dim(collected, slot_index, 0, keepdims=False)  24.9 us
    dynamic_update_slice x23, other arithmetic, advance(): lax.dynamic_update_index_in_dim(collected, jnp.where(arrived, outgoing, p...  24 us
    another operation x1, loops' own time, per_device(): lax.scan(cycle_step, carried, jnp.arange(section_count - 1, step_count -...  20.6 us
  transfers between devices with their start and end apart: 38, of which 38 were waited for; matrix products, arithmetic and copies ran while one was open for 2% of the time, Pallas kernels for 0%

profile of v1, /device:TPU:160, one launch (start us, length us, event | category | flops | bytes accessed | tf_op | source)
XLA Modules:
  0.0 923.4 jit_solution(11807377221036130820)
XLA Ops:
  5.5 9.8 %all-to-all-start = ((bf16[8,1,1,128,4096]{4,3,2,1,0:T(8,128)(2,1)}), bf16[8,1,1,128,4096]{4,3,2,1,0:T(8,128)(2,1)}, u32[]{:S(2)}, u32[]{:S(2)}) async-start(bf16[8,1,1,128,4096]{4,3,2,1,0:T(8,128)(2,1)} %stack.2), calls=%async_computation | async-start | bytes 16777216 | tf_op jit(solution)/shard_map/all_to_all | solution.py:10
  15.3 164.3 %all-to-all-done = bf16[8,1,1,128,4096]{4,3,2,1,0:T(8,128)(2,1)} async-done(((bf16[8,1,1,128,4096]{4,3,2,1,0:T(8,128)(2,1)}), bf16[8,1,1,128,4096]{4,3,2,1,0:T(8,128)(2,1)}, u32[]{:S(2)}, u32[]{:S(2)}) %all-to-all-start) | async-done | bytes 8388640 | tf_op jit(solution)/shard_map/all_to_all | solution.py:10
  180.8 247.6 %while.40 = (s32[]{:T(128)}, bf16[64,4096]{1,0:T(8,128)(2,1)S(1)}, bf16[64,4096]{1,0:T(8,128)(2,1)S(1)}, bf16[2,64,4096]{2,1,0:T(8,128)(2,1)}, s32[7]{0:T(128)S(...) while((s32[]{:T(128)}, bf16[64,4096]{1,0:T(8,128)(2,1)S(1)}, ...), condition=%wide.region_4.5_spmd.clone, body=%wide.region_0.4_spmd.clone.sunk | while | flops 557416960 | bytes 36344376 | solution.py:107
  183.2 22.2 %collective-permute-start.2 = (bf16[64,4096]{1,0:T(8,128)(2,1)S(1)}, bf16[64,4096]{1,0:T(8,128)(2,1)S(1)}, u32[]{:S(2)}, u32[]{:S(2)}) collective-permute-start(bf16[64,4096]{1,0:T(8,128)(2,1)S(1)} %get-tuple-element.1181), channel_id=1, source_target_pairs={{0,32},{32,64},{64,96},{96,128},{128,160},{160,192},{192,224},{1,3... | collective-permute-start | bytes 1572872 | tf_op jit(solution)/shard_map/while/body/eval_jaxpr/ppermute | solution.py:21
  208.2 23.6 %collective-permute-done.2 = bf16[64,4096]{1,0:T(8,128)(2,1)S(1)} collective-permute-done((bf16[64,4096]{1,0:T(8,128)(2,1)S(1)}, bf16[64,4096]{1,0:T(8,128)(2,1)S(1)}, u32[]{:S(2)}, u32[]{:S(2)}) %collective-permute-start.2) | collective-permute-done | bytes 524320 | tf_op jit(solution)/shard_map/while/body/eval_jaxpr/ppermute | solution.py:21
  239.0 28.5 %collective-permute-done.2 = bf16[64,4096]{1,0:T(8,128)(2,1)S(1)} collective-permute-done((bf16[64,4096]{1,0:T(8,128)(2,1)S(1)}, bf16[64,4096]{1,0:T(8,128)(2,1)S(1)}, u32[]{:S(2)}, u32[]{:S(2)}) %collective-permute-start.2) | collective-permute-done | bytes 524320 | tf_op jit(solution)/shard_map/while/body/eval_jaxpr/ppermute | solution.py:21
  274.7 23.0 %collective-permute-done.2 = bf16[64,4096]{1,0:T(8,128)(2,1)S(1)} collective-permute-done((bf16[64,4096]{1,0:T(8,128)(2,1)S(1)}, bf16[64,4096]{1,0:T(8,128)(2,1)S(1)}, u32[]{:S(2)}, u32[]{:S(2)}) %collective-permute-start.2) | collective-permute-done | bytes 524320 | tf_op jit(solution)/shard_map/while/body/eval_jaxpr/ppermute | solution.py:21
  304.9 17.1 %collective-permute-done.2 = bf16[64,4096]{1,0:T(8,128)(2,1)S(1)} collective-permute-done((bf16[64,4096]{1,0:T(8,128)(2,1)S(1)}, bf16[64,4096]{1,0:T(8,128)(2,1)S(1)}, u32[]{:S(2)}, u32[]{:S(2)}) %collective-permute-start.2) | collective-permute-done | bytes 524320 | tf_op jit(solution)/shard_map/while/body/eval_jaxpr/ppermute | solution.py:21
  333.9 27.5 %collective-permute-done.2 = bf16[64,4096]{1,0:T(8,128)(2,1)S(1)} collective-permute-done((bf16[64,4096]{1,0:T(8,128)(2,1)S(1)}, bf16[64,4096]{1,0:T(8,128)(2,1)S(1)}, u32[]{:S(2)}, u32[]{:S(2)}) %collective-permute-start.2) | collective-permute-done | bytes 524320 | tf_op jit(solution)/shard_map/while/body/eval_jaxpr/ppermute | solution.py:21
  373.3 22.4 %collective-permute-done.2 = bf16[64,4096]{1,0:T(8,128)(2,1)S(1)} collective-permute-done((bf16[64,4096]{1,0:T(8,128)(2,1)S(1)}, bf16[64,4096]{1,0:T(8,128)(2,1)S(1)}, u32[]{:S(2)}, u32[]{:S(2)}) %collective-permute-start.2) | collective-permute-done | bytes 524320 | tf_op jit(solution)/shard_map/while/body/eval_jaxpr/ppermute | solution.py:21
  407.6 20.8 %collective-permute-done.2 = bf16[64,4096]{1,0:T(8,128)(2,1)S(1)} collective-permute-done((bf16[64,4096]{1,0:T(8,128)(2,1)S(1)}, bf16[64,4096]{1,0:T(8,128)(2,1)S(1)}, u32[]{:S(2)}, u32[]{:S(2)}) %collective-permute-start.2) | collective-permute-done | bytes 524320 | tf_op jit(solution)/shard_map/while/body/eval_jaxpr/ppermute | solution.py:21
  428.4 491.8 %while.39 = (s32[]{:T(128)}, bf16[64,4096]{1,0:T(8,128)(2,1)S(1)}, bf16[64,4096]{1,0:T(8,128)(2,1)S(1)}, bf16[2,64,4096]{2,1,0:T(8,128)(2,1)}, s32[15]{0:T(128)S...) while((s32[]{:T(128)}, bf16[64,4096]{1,0:T(8,128)(2,1)S(1)}, ...), condition=%wide.region_9.10_spmd, body=%wide.region_5.9_spmd.sunk | while | flops 557154816 | bytes 38441560 | solution.py:110
  444.2 13.3 %collective-permute-done.1 = bf16[64,4096]{1,0:T(8,128)(2,1)S(1)} collective-permute-done((bf16[64,4096]{1,0:T(8,128)(2,1)S(1)}, bf16[64,4096]{1,0:T(8,128)(2,1)S(1)}, u32[]{:S(2)}, u32[]{:S(2)}) %collective-permute-start.1) | collective-permute-done | bytes 524320 | tf_op jit(solution)/shard_map/while/body/eval_jaxpr/ppermute | solution.py:21
  457.5 10.1 %collective-permute-done = bf16[64,4096]{1,0:T(8,128)(2,1)S(1)} collective-permute-done((bf16[64,4096]{1,0:T(8,128)(2,1)S(1)}, bf16[64,4096]{1,0:T(8,128)(2,1)S(1)}, u32[]{:S(2)}, u32[]{:S(2)}) %collective-permute-start) | collective-permute-done | bytes 524320 | tf_op jit(solution)/shard_map/while/body/eval_jaxpr/ppermute | solution.py:21
  483.3 13.4 %collective-permute-done.1 = bf16[64,4096]{1,0:T(8,128)(2,1)S(1)} collective-permute-done((bf16[64,4096]{1,0:T(8,128)(2,1)S(1)}, bf16[64,4096]{1,0:T(8,128)(2,1)S(1)}, u32[]{:S(2)}, u32[]{:S(2)}) %collective-permute-start.1) | collective-permute-done | bytes 524320 | tf_op jit(solution)/shard_map/while/body/eval_jaxpr/ppermute | solution.py:21
  496.8 10.1 %collective-permute-done = bf16[64,4096]{1,0:T(8,128)(2,1)S(1)} collective-permute-done((bf16[64,4096]{1,0:T(8,128)(2,1)S(1)}, bf16[64,4096]{1,0:T(8,128)(2,1)S(1)}, u32[]{:S(2)}, u32[]{:S(2)}) %collective-permute-start) | collective-permute-done | bytes 524320 | tf_op jit(solution)/shard_map/while/body/eval_jaxpr/ppermute | solution.py:21
  522.7 16.8 %collective-permute-done.1 = bf16[64,4096]{1,0:T(8,128)(2,1)S(1)} collective-permute-done((bf16[64,4096]{1,0:T(8,128)(2,1)S(1)}, bf16[64,4096]{1,0:T(8,128)(2,1)S(1)}, u32[]{:S(2)}, u32[]{:S(2)}) %collective-permute-start.1) | collective-permute-done | bytes 524320 | tf_op jit(solution)/shard_map/while/body/eval_jaxpr/ppermute | solution.py:21
  539.4 10.4 %collective-permute-done = bf16[64,4096]{1,0:T(8,128)(2,1)S(1)} collective-permute-done((bf16[64,4096]{1,0:T(8,128)(2,1)S(1)}, bf16[64,4096]{1,0:T(8,128)(2,1)S(1)}, u32[]{:S(2)}, u32[]{:S(2)}) %collective-permute-start) | collective-permute-done | bytes 524320 | tf_op jit(solution)/shard_map/while/body/eval_jaxpr/ppermute | solution.py:21
  565.6 9.9 %collective-permute-done.1 = bf16[64,4096]{1,0:T(8,128)(2,1)S(1)} collective-permute-done((bf16[64,4096]{1,0:T(8,128)(2,1)S(1)}, bf16[64,4096]{1,0:T(8,128)(2,1)S(1)}, u32[]{:S(2)}, u32[]{:S(2)}) %collective-permute-start.1) | collective-permute-done | bytes 524320 | tf_op jit(solution)/shard_map/while/body/eval_jaxpr/ppermute | solution.py:21
  575.5 9.3 %collective-permute-done = bf16[64,4096]{1,0:T(8,128)(2,1)S(1)} collective-permute-done((bf16[64,4096]{1,0:T(8,128)(2,1)S(1)}, bf16[64,4096]{1,0:T(8,128)(2,1)S(1)}, u32[]{:S(2)}, u32[]{:S(2)}) %collective-permute-start) | collective-permute-done | bytes 524320 | tf_op jit(solution)/shard_map/while/body/eval_jaxpr/ppermute | solution.py:21
  600.5 19.0 %collective-permute-done.1 = bf16[64,4096]{1,0:T(8,128)(2,1)S(1)} collective-permute-done((bf16[64,4096]{1,0:T(8,128)(2,1)S(1)}, bf16[64,4096]{1,0:T(8,128)(2,1)S(1)}, u32[]{:S(2)}, u32[]{:S(2)}) %collective-permute-start.1) | collective-permute-done | bytes 524320 | tf_op jit(solution)/shard_map/while/body/eval_jaxpr/ppermute | solution.py:21
  619.5 10.1 %collective-permute-done = bf16[64,4096]{1,0:T(8,128)(2,1)S(1)} collective-permute-done((bf16[64,4096]{1,0:T(8,128)(2,1)S(1)}, bf16[64,4096]{1,0:T(8,128)(2,1)S(1)}, u32[]{:S(2)}, u32[]{:S(2)}) %collective-permute-start) | collective-permute-done | bytes 524320 | tf_op jit(solution)/shard_map/while/body/eval_jaxpr/ppermute | solution.py:21
  645.3 9.9 %collective-permute-done.1 = bf16[64,4096]{1,0:T(8,128)(2,1)S(1)} collective-permute-done((bf16[64,4096]{1,0:T(8,128)(2,1)S(1)}, bf16[64,4096]{1,0:T(8,128)(2,1)S(1)}, u32[]{:S(2)}, u32[]{:S(2)}) %collective-permute-start.1) | collective-permute-done | bytes 524320 | tf_op jit(solution)/shard_map/while/body/eval_jaxpr/ppermute | solution.py:21
  655.3 10.4 %collective-permute-done = bf16[64,4096]{1,0:T(8,128)(2,1)S(1)} collective-permute-done((bf16[64,4096]{1,0:T(8,128)(2,1)S(1)}, bf16[64,4096]{1,0:T(8,128)(2,1)S(1)}, u32[]{:S(2)}, u32[]{:S(2)}) %collective-permute-start) | collective-permute-done | bytes 524320 | tf_op jit(solution)/shard_map/while/body/eval_jaxpr/ppermute | solution.py:21
  (324 shorter events, 465.8 us)
Async XLA Ops:
  5.5 174.1 %all-to-all-start = ((bf16[8,1,1,128,4096]{4,3,2,1,0:T(8,128)(2,1)}), bf16[8,1,1,128,4096]{4,3,2,1,0:T(8,128)(2,1)}, u32[]{:S(2)}, u32[]{:S(2)}) async-start(bf16[8,1,1,128,4096]{4,3,2,1,0:T(8,128)(2,1)} %stack.2), calls=%async_computation | async-start | bytes 16777216 | tf_op jit(solution)/shard_map/all_to_all | solution.py:10
  183.2 48.6 %collective-permute-start.2 = (bf16[64,4096]{1,0:T(8,128)(2,1)S(1)}, bf16[64,4096]{1,0:T(8,128)(2,1)S(1)}, u32[]{:S(2)}, u32[]{:S(2)}) collective-permute-start(bf16[64,4096]{1,0:T(8,128)(2,1)S(1)} %get-tuple-element.1181), channel_id=1, source_target_pairs={{0,32},{32,64},{64,96},{96,128},{128,160},{160,192},{192,224},{1,3... | collective-permute-start | bytes 1572872 | tf_op jit(solution)/shard_map/while/body/eval_jaxpr/ppermute | solution.py:21
  234.2 33.3 %collective-permute-start.2 = (bf16[64,4096]{1,0:T(8,128)(2,1)S(1)}, bf16[64,4096]{1,0:T(8,128)(2,1)S(1)}, u32[]{:S(2)}, u32[]{:S(2)}) collective-permute-start(bf16[64,4096]{1,0:T(8,128)(2,1)S(1)} %get-tuple-element.1181), channel_id=1, source_target_pairs={{0,32},{32,64},{64,96},{96,128},{128,160},{160,192},{192,224},{1,3... | collective-permute-start | bytes 1572872 | tf_op jit(solution)/shard_map/while/body/eval_jaxpr/ppermute | solution.py:21
  269.8 27.9 %collective-permute-start.2 = (bf16[64,4096]{1,0:T(8,128)(2,1)S(1)}, bf16[64,4096]{1,0:T(8,128)(2,1)S(1)}, u32[]{:S(2)}, u32[]{:S(2)}) collective-permute-start(bf16[64,4096]{1,0:T(8,128)(2,1)S(1)} %get-tuple-element.1181), channel_id=1, source_target_pairs={{0,32},{32,64},{64,96},{96,128},{128,160},{160,192},{192,224},{1,3... | collective-permute-start | bytes 1572872 | tf_op jit(solution)/shard_map/while/body/eval_jaxpr/ppermute | solution.py:21
  300.1 21.9 %collective-permute-start.2 = (bf16[64,4096]{1,0:T(8,128)(2,1)S(1)}, bf16[64,4096]{1,0:T(8,128)(2,1)S(1)}, u32[]{:S(2)}, u32[]{:S(2)}) collective-permute-start(bf16[64,4096]{1,0:T(8,128)(2,1)S(1)} %get-tuple-element.1181), channel_id=1, source_target_pairs={{0,32},{32,64},{64,96},{96,128},{128,160},{160,192},{192,224},{1,3... | collective-permute-start | bytes 1572872 | tf_op jit(solution)/shard_map/while/body/eval_jaxpr/ppermute | solution.py:21
  329.1 32.3 %collective-permute-start.2 = (bf16[64,4096]{1,0:T(8,128)(2,1)S(1)}, bf16[64,4096]{1,0:T(8,128)(2,1)S(1)}, u32[]{:S(2)}, u32[]{:S(2)}) collective-permute-start(bf16[64,4096]{1,0:T(8,128)(2,1)S(1)} %get-tuple-element.1181), channel_id=1, source_target_pairs={{0,32},{32,64},{64,96},{96,128},{128,160},{160,192},{192,224},{1,3... | collective-permute-start | bytes 1572872 | tf_op jit(solution)/shard_map/while/body/eval_jaxpr/ppermute | solution.py:21
  368.5 27.2 %collective-permute-start.2 = (bf16[64,4096]{1,0:T(8,128)(2,1)S(1)}, bf16[64,4096]{1,0:T(8,128)(2,1)S(1)}, u32[]{:S(2)}, u32[]{:S(2)}) collective-permute-start(bf16[64,4096]{1,0:T(8,128)(2,1)S(1)} %get-tuple-element.1181), channel_id=1, source_target_pairs={{0,32},{32,64},{64,96},{96,128},{128,160},{160,192},{192,224},{1,3... | collective-permute-start | bytes 1572872 | tf_op jit(solution)/shard_map/while/body/eval_jaxpr/ppermute | solution.py:21
  402.8 25.6 %collective-permute-start.2 = (bf16[64,4096]{1,0:T(8,128)(2,1)S(1)}, bf16[64,4096]{1,0:T(8,128)(2,1)S(1)}, u32[]{:S(2)}, u32[]{:S(2)}) collective-permute-start(bf16[64,4096]{1,0:T(8,128)(2,1)S(1)} %get-tuple-element.1181), channel_id=1, source_target_pairs={{0,32},{32,64},{64,96},{96,128},{128,160},{160,192},{192,224},{1,3... | collective-permute-start | bytes 1572872 | tf_op jit(solution)/shard_map/while/body/eval_jaxpr/ppermute | solution.py:21
  438.3 19.2 %collective-permute-start.1 = (bf16[64,4096]{1,0:T(8,128)(2,1)S(1)}, bf16[64,4096]{1,0:T(8,128)(2,1)S(1)}, u32[]{:S(2)}, u32[]{:S(2)}) collective-permute-start(bf16[64,4096]{1,0:T(8,128)(2,1)S(1)} %get-tuple-element.1015), channel_id=1, source_target_pairs={{32,0},{64,32},{96,64},{128,96},{160,128},{192,160},{224,192},{33,... | collective-permute-start | bytes 1572872 | tf_op jit(solution)/shard_map/while/body/eval_jaxpr/ppermute | solution.py:21
  440.2 27.4 %collective-permute-start = (bf16[64,4096]{1,0:T(8,128)(2,1)S(1)}, bf16[64,4096]{1,0:T(8,128)(2,1)S(1)}, u32[]{:S(2)}, u32[]{:S(2)}) collective-permute-start(bf16[64,4096]{1,0:T(8,128)(2,1)S(1)} %get-tuple-element.1180), channel_id=1, source_target_pairs={{0,32},{32,64},{64,96},{96,128},{128,160},{160,192},{192,224},{1,3... | collective-permute-start | bytes 1572872 | tf_op jit(solution)/shard_map/while/body/eval_jaxpr/ppermute | solution.py:21
  477.5 19.3 %collective-permute-start.1 = (bf16[64,4096]{1,0:T(8,128)(2,1)S(1)}, bf16[64,4096]{1,0:T(8,128)(2,1)S(1)}, u32[]{:S(2)}, u32[]{:S(2)}) collective-permute-start(bf16[64,4096]{1,0:T(8,128)(2,1)S(1)} %get-tuple-element.1015), channel_id=1, source_target_pairs={{32,0},{64,32},{96,64},{128,96},{160,128},{192,160},{224,192},{33,... | collective-permute-start | bytes 1572872 | tf_op jit(solution)/shard_map/while/body/eval_jaxpr/ppermute | solution.py:21
  479.4 27.5 %collective-permute-start = (bf16[64,4096]{1,0:T(8,128)(2,1)S(1)}, bf16[64,4096]{1,0:T(8,128)(2,1)S(1)}, u32[]{:S(2)}, u32[]{:S(2)}) collective-permute-start(bf16[64,4096]{1,0:T(8,128)(2,1)S(1)} %get-tuple-element.1180), channel_id=1, source_target_pairs={{0,32},{32,64},{64,96},{96,128},{128,160},{160,192},{192,224},{1,3... | collective-permute-start | bytes 1572872 | tf_op jit(solution)/shard_map/while/body/eval_jaxpr/ppermute | solution.py:21
  516.8 22.6 %collective-permute-start.1 = (bf16[64,4096]{1,0:T(8,128)(2,1)S(1)}, bf16[64,4096]{1,0:T(8,128)(2,1)S(1)}, u32[]{:S(2)}, u32[]{:S(2)}) collective-permute-start(bf16[64,4096]{1,0:T(8,128)(2,1)S(1)} %get-tuple-element.1015), channel_id=1, source_target_pairs={{32,0},{64,32},{96,64},{128,96},{160,128},{192,160},{224,192},{33,... | collective-permute-start | bytes 1572872 | tf_op jit(solution)/shard_map/while/body/eval_jaxpr/ppermute | solution.py:21
  518.7 31.1 %collective-permute-start = (bf16[64,4096]{1,0:T(8,128)(2,1)S(1)}, bf16[64,4096]{1,0:T(8,128)(2,1)S(1)}, u32[]{:S(2)}, u32[]{:S(2)}) collective-permute-start(bf16[64,4096]{1,0:T(8,128)(2,1)S(1)} %get-tuple-element.1180), channel_id=1, source_target_pairs={{0,32},{32,64},{64,96},{96,128},{128,160},{160,192},{192,224},{1,3... | collective-permute-start | bytes 1572872 | tf_op jit(solution)/shard_map/while/body/eval_jaxpr/ppermute | solution.py:21
  561.7 23.1 %collective-permute-start = (bf16[64,4096]{1,0:T(8,128)(2,1)S(1)}, bf16[64,4096]{1,0:T(8,128)(2,1)S(1)}, u32[]{:S(2)}, u32[]{:S(2)}) collective-permute-start(bf16[64,4096]{1,0:T(8,128)(2,1)S(1)} %get-tuple-element.1180), channel_id=1, source_target_pairs={{0,32},{32,64},{64,96},{96,128},{128,160},{160,192},{192,224},{1,3... | collective-permute-start | bytes 1572872 | tf_op jit(solution)/shard_map/while/body/eval_jaxpr/ppermute | solution.py:21
  594.7 24.8 %collective-permute-start.1 = (bf16[64,4096]{1,0:T(8,128)(2,1)S(1)}, bf16[64,4096]{1,0:T(8,128)(2,1)S(1)}, u32[]{:S(2)}, u32[]{:S(2)}) collective-permute-start(bf16[64,4096]{1,0:T(8,128)(2,1)S(1)} %get-tuple-element.1015), channel_id=1, source_target_pairs={{32,0},{64,32},{96,64},{128,96},{160,128},{192,160},{224,192},{33,... | collective-permute-start | bytes 1572872 | tf_op jit(solution)/shard_map/while/body/eval_jaxpr/ppermute | solution.py:21
  596.6 33.0 %collective-permute-start = (bf16[64,4096]{1,0:T(8,128)(2,1)S(1)}, bf16[64,4096]{1,0:T(8,128)(2,1)S(1)}, u32[]{:S(2)}, u32[]{:S(2)}) collective-permute-start(bf16[64,4096]{1,0:T(8,128)(2,1)S(1)} %get-tuple-element.1180), channel_id=1, source_target_pairs={{0,32},{32,64},{64,96},{96,128},{128,160},{160,192},{192,224},{1,3... | collective-permute-start | bytes 1572872 | tf_op jit(solution)/shard_map/while/body/eval_jaxpr/ppermute | solution.py:21
  641.4 24.3 %collective-permute-start = (bf16[64,4096]{1,0:T(8,128)(2,1)S(1)}, bf16[64,4096]{1,0:T(8,128)(2,1)S(1)}, u32[]{:S(2)}, u32[]{:S(2)}) collective-permute-start(bf16[64,4096]{1,0:T(8,128)(2,1)S(1)} %get-tuple-element.1180), channel_id=1, source_target_pairs={{0,32},{32,64},{64,96},{96,128},{128,160},{160,192},{192,224},{1,3... | collective-permute-start | bytes 1572872 | tf_op jit(solution)/shard_map/while/body/eval_jaxpr/ppermute | solution.py:21
  677.5 19.2 %collective-permute-start = (bf16[64,4096]{1,0:T(8,128)(2,1)S(1)}, bf16[64,4096]{1,0:T(8,128)(2,1)S(1)}, u32[]{:S(2)}, u32[]{:S(2)}) collective-permute-start(bf16[64,4096]{1,0:T(8,128)(2,1)S(1)} %get-tuple-element.1180), channel_id=1, source_target_pairs={{0,32},{32,64},{64,96},{96,128},{128,160},{160,192},{192,224},{1,3... | collective-permute-start | bytes 1572872 | tf_op jit(solution)/shard_map/while/body/eval_jaxpr/ppermute | solution.py:21
  708.5 18.4 %collective-permute-start = (bf16[64,4096]{1,0:T(8,128)(2,1)S(1)}, bf16[64,4096]{1,0:T(8,128)(2,1)S(1)}, u32[]{:S(2)}, u32[]{:S(2)}) collective-permute-start(bf16[64,4096]{1,0:T(8,128)(2,1)S(1)} %get-tuple-element.1180), channel_id=1, source_target_pairs={{0,32},{32,64},{64,96},{96,128},{128,160},{160,192},{192,224},{1,3... | collective-permute-start | bytes 1572872 | tf_op jit(solution)/shard_map/while/body/eval_jaxpr/ppermute | solution.py:21
  738.7 17.5 %collective-permute-start = (bf16[64,4096]{1,0:T(8,128)(2,1)S(1)}, bf16[64,4096]{1,0:T(8,128)(2,1)S(1)}, u32[]{:S(2)}, u32[]{:S(2)}) collective-permute-start(bf16[64,4096]{1,0:T(8,128)(2,1)S(1)} %get-tuple-element.1180), channel_id=1, source_target_pairs={{0,32},{32,64},{64,96},{96,128},{128,160},{160,192},{192,224},{1,3... | collective-permute-start | bytes 1572872 | tf_op jit(solution)/shard_map/while/body/eval_jaxpr/ppermute | solution.py:21
  768.0 17.1 %collective-permute-start = (bf16[64,4096]{1,0:T(8,128)(2,1)S(1)}, bf16[64,4096]{1,0:T(8,128)(2,1)S(1)}, u32[]{:S(2)}, u32[]{:S(2)}) collective-permute-start(bf16[64,4096]{1,0:T(8,128)(2,1)S(1)} %get-tuple-element.1180), channel_id=1, source_target_pairs={{0,32},{32,64},{64,96},{96,128},{128,160},{160,192},{192,224},{1,3... | collective-permute-start | bytes 1572872 | tf_op jit(solution)/shard_map/while/body/eval_jaxpr/ppermute | solution.py:21
  796.9 17.1 %collective-permute-start = (bf16[64,4096]{1,0:T(8,128)(2,1)S(1)}, bf16[64,4096]{1,0:T(8,128)(2,1)S(1)}, u32[]{:S(2)}, u32[]{:S(2)}) collective-permute-start(bf16[64,4096]{1,0:T(8,128)(2,1)S(1)} %get-tuple-element.1180), channel_id=1, source_target_pairs={{0,32},{32,64},{64,96},{96,128},{128,160},{160,192},{192,224},{1,3... | collective-permute-start | bytes 1572872 | tf_op jit(solution)/shard_map/while/body/eval_jaxpr/ppermute | solution.py:21
  825.8 17.1 %collective-permute-start = (bf16[64,4096]{1,0:T(8,128)(2,1)S(1)}, bf16[64,4096]{1,0:T(8,128)(2,1)S(1)}, u32[]{:S(2)}, u32[]{:S(2)}) collective-permute-start(bf16[64,4096]{1,0:T(8,128)(2,1)S(1)} %get-tuple-element.1180), channel_id=1, source_target_pairs={{0,32},{32,64},{64,96},{96,128},{128,160},{160,192},{192,224},{1,3... | collective-permute-start | bytes 1572872 | tf_op jit(solution)/shard_map/while/body/eval_jaxpr/ppermute | solution.py:21
  (33 other events, 771.2 us)
